TPU v7x, 32 devices: a whole 2x2x4 slice. The times are simulated.
32 devices in a mesh: section: 2 (over x), seq: 8 (over z, y), rep: 2 (over core).
Axes of the slice: x: 2, y: 2, z: 4, core: 2. Of those that a mesh axis runs over, the one named last changes fastest.
Arguments:
- queries: bfloat16 [512, 2560], P('seq', ('section', 'rep')), may hold values from -5 to 5
- keys: bfloat16 [512, 2560], P('seq', ('section', 'rep')), may hold values from -5 to 5
- values: bfloat16 [512, 2560], P('seq', ('section', 'rep')), may hold values from -6 to 6
- block_order: int32 [16], replicated, may hold values from 0 to 15, each once
- wo: bfloat16 [2560, 5120], P(('section', 'rep'), 'seq'), may hold values from -0.125 to 0.125
- resid: bfloat16 [4, 5120, 128], P(('section', 'rep'), 'seq'), may hold values from -60 to 60
- gain: bfloat16 [5120], P('seq'), may hold values from 0.099609375 to 1.8984375
- w_gate: bfloat16 [13824, 5120], P('seq'), may hold values from -0.078125 to 0.078125
- w_up: bfloat16 [13824, 5120], P('seq'), may hold values from -0.078125 to 0.078125
- w_down: bfloat16 [13824, 5120], P('seq'), may hold values from -0.0625 to 0.0625
Outputs:
- mixed: bfloat16 [4, 5120, 128], P(('section', 'rep'), 'seq')
Inputs may be any that keep to these rules, and one draw needn't show every extreme that they name: `block_order`: each number once.
All inputs are finite; a program needn't handle non-finite values.
Results may differ from a plain program's by a relative error of at most 0.0055.
Values may be sent and summed in bfloat16 or wider, within the bound.
A program may use at most 128 MiB of HBM per device.

v0:
```python
import jax
import jax.numpy as jnp
from jax import lax
from jax.sharding import PartitionSpec as P

D = 5120
HEAD_DIM = 128


def key_positions(order, start, count, block_rows):
    row_ids = start + jnp.arange(count, dtype=jnp.int32)
    owners = row_ids // block_rows
    match = owners[:, None] == jnp.arange(order.shape[0], dtype=jnp.int32)[None, :]
    first = jnp.sum(jnp.where(match, order[None, :], 0), axis=1)
    return first * block_rows + row_ids % block_rows


def on_device(queries, keys, values, block_order, wo, resid, gain, w_gate, w_up, w_down):
    seq_dev = queries.shape[0]
    heads_dev = queries.shape[1] // HEAD_DIM
    groups = lax.axis_size("section") * lax.axis_size("rep")
    n_seq = lax.axis_size("seq")
    sub_rows = seq_dev // groups
    block_rows = seq_dev // 2
    query_start = lax.axis_index("seq") * seq_dev
    query_pos = key_positions(block_order, query_start, seq_dev, block_rows)
    query_heads = queries.reshape(seq_dev, heads_dev, HEAD_DIM)
    scale = HEAD_DIM ** (-0.5)
    running_max = jnp.full((seq_dev, heads_dev), -1e30, jnp.float32)
    key_piece = lax.all_gather(keys, "seq", axis=0, tiled=True)
    value_piece = lax.all_gather(values, "seq", axis=0, tiled=True)
    count = key_piece.shape[0]
    key_pos = key_positions(block_order, jnp.int32(0), count, block_rows)
    scores = (
        jnp.einsum(
            "qhd,khd->qhk",
            query_heads,
            key_piece.reshape(count, heads_dev, HEAD_DIM),
            preferred_element_type=jnp.float32,
        )
        * scale
    )
    visible = (key_pos[None, :] <= query_pos[:, None])[:, None, :]
    new_max = jnp.maximum(running_max, jnp.max(jnp.where(visible, scores, -1e30), axis=-1))
    probs = jnp.where(visible, jnp.exp(scores - new_max[..., None]), 0.0)
    total = jnp.sum(probs, axis=-1)
    weighted = jnp.einsum(
        "qhk,khd->qhd",
        probs.astype(jnp.bfloat16),
        value_piece.reshape(count, heads_dev, HEAD_DIM),
        preferred_element_type=jnp.float32,
    )
    running_max, total, weighted = (new_max, total, weighted)
    attended = (
        (weighted / total[..., None]).astype(jnp.bfloat16).reshape(seq_dev, heads_dev * HEAD_DIM)
    )
    columns = wo.shape[1]
    token_count = n_seq * sub_rows
    parts = attended.reshape(groups, sub_rows, heads_dev * HEAD_DIM)
    group_rows = lax.all_to_all(parts, ("section", "rep"), split_axis=0, concat_axis=2, tiled=True)
    wo_columns = lax.all_gather(wo, ("section", "rep"), axis=0, tiled=True)
    piece = lax.all_gather(group_rows, "seq", axis=0, tiled=True)
    flat = piece.reshape(piece.shape[0] * piece.shape[1], piece.shape[2])
    product = jnp.dot(flat, wo_columns, preferred_element_type=jnp.float32)
    projected = product.reshape(piece.shape[0], piece.shape[1], columns)
    projected_cols = projected.reshape(token_count, columns).T
    carried = resid.reshape(columns, token_count).astype(jnp.float32) + projected_cols
    squares = lax.psum(jnp.sum(carried * carried, axis=0), "seq")
    normed = (
        carried * lax.rsqrt(squares / D + 1e-05)[None, :] * gain.astype(jnp.float32)[:, None]
    ).astype(jnp.bfloat16)
    piece = lax.all_gather(normed, "seq", axis=0, tiled=True)
    gate_sum = jnp.dot(w_gate, piece, preferred_element_type=jnp.float32)
    up_sum = jnp.dot(w_up, piece, preferred_element_type=jnp.float32)
    hidden = (jax.nn.silu(gate_sum) * up_sum).astype(jnp.bfloat16)
    term = lax.dot_general(
        w_down, hidden, (((0,), (0,)), ((), ())), preferred_element_type=jnp.float32
    )
    down = lax.psum_scatter(term, "seq", scatter_dimension=0, tiled=True)
    return (carried + down).astype(jnp.bfloat16).reshape(resid.shape)


def solution(mesh):
    return jax.shard_map(
        on_device,
        mesh=mesh,
        in_specs=(
            P("seq", ("section", "rep")),
            P("seq", ("section", "rep")),
            P("seq", ("section", "rep")),
            P(),
            P(("section", "rep"), "seq"),
            P(("section", "rep"), "seq", None),
            P("seq"),
            P("seq", None),
            P("seq", None),
            P("seq", None),
        ),
        out_specs=P(("section", "rep"), "seq", None),
        check_vma=False,
    )
```

profile of v0, /device:TPU:24, one launch (start us, length us, event | category | flops | bytes accessed | tf_op | source)
XLA Modules:
  0.0 285.3 jit_solution(9217807981591576571)
XLA Ops:
  6.5 0.0 copy-start
  6.5 0.0 copy-start.5
  6.5 0.0 all-gather.3.cloned.1.call-start
  6.5 0.7 all-gather.3.cloned.1.call-update
  7.3 29.5 %all_gather.15 = bf16[512,640]{1,0:T(8,128)(2,1)S(1)} all-gather(bf16[64,640]{1,0:T(8,128)(2,1)} %param.11), channel_id=1, replica_groups=mesh['section'=2,'seq'=8,'rep'=2] {'seq'}, dimensions={0}, use_global_device_ids=true | all-gather | bytes 737280 | tf_op jit(solution)/shard_map/all_gather | solution.py:30
  36.7 0.3 copy.33
  37.0 0.0 copy-start.3
  37.0 31.6 %all_gather.16 = bf16[512,640]{1,0:T(8,128)(2,1)S(1)} all-gather(bf16[64,640]{1,0:T(8,128)(2,1)} %param.12), channel_id=1, replica_groups=mesh['section'=2,'seq'=8,'rep'=2] {'seq'}, dimensions={0}, use_global_device_ids=true | all-gather | bytes 737280 | tf_op jit(solution)/shard_map/all_gather | solution.py:31
  68.6 0.0 copy-start.4
  68.6 0.3 copy.36
  68.9 0.0 copy-done.5
  68.9 0.1 select_reduce_fusion.2
  69.0 0.1 select_reduce_fusion.1
  69.1 0.1 broadcast_compare_fusion
  69.2 0.0 copy-done
  69.2 0.3 select_reduce_fusion
  69.5 0.3 fusion.6
  69.8 0.4 fusion.5
  70.2 0.1 copy.38
  70.2 0.7 reshape_reshape.3
  71.0 3.3 %all-to-all-start = ((bf16[4,16,640]{2,1,0:T(8,128)(2,1)}), bf16[4,16,640]{2,1,0:T(8,128)(2,1)S(1)}, u32[]{:S(2)}, u32[]{:S(2)}) async-start(bf16[4,16,640]{2,1,0:T(8,128)(2,1)} %reshape_reshape.3), calls=%async_computation | async-start | bytes 163840 | tf_op jit(solution)/shard_map/all_to_all | solution.py:60
  74.3 0.0 all-gather.5.cloned.1.call-start
  74.3 0.0 copy-done.3
  74.3 0.2 copy.32
  74.5 0.0 copy-done.4
  74.5 3.9 %all-to-all-done = bf16[4,16,640]{2,1,0:T(8,128)(2,1)S(1)} async-done(((bf16[4,16,640]{2,1,0:T(8,128)(2,1)}), bf16[4,16,640]{2,1,0:T(8,128)(2,1)S(1)}, u32[]{:S(2)}, u32[]{:S(2)}) %all-to-all-start) | async-done | bytes 81952 | tf_op jit(solution)/shard_map/all_to_all | solution.py:60
  78.5 31.7 %all_gather.17 = bf16[8,16,2560]{2,1,0:T(8,128)(2,1)S(1)} all-gather(bf16[1,16,2560]{2,1,0:T(8,128)(2,1)S(1)} %bitcast.59), channel_id=1, replica_groups=mesh['section'=2,'seq'=8,'rep'=2] {'seq'}, dimensions={0}, use_global_device_ids=true | all-gather | bytes 737280 | tf_op jit(solution)/shard_map/all_gather | solution.py:62
  110.1 0.0 all-gather.3.cloned.1.call-done
  110.1 2.7 multiply_reduce_fusion
  112.8 19.7 %psum.7 = f32[128]{0:T(128)S(1)} all-reduce(f32[128]{0:T(128)S(1)} %get-tuple-element.7), channel_id=1, replica_groups=mesh['section'=2,'seq'=8,'rep'=2] {'seq'}, use_global_device_ids=true, to_apply=%region_5.6 | all-reduce | flops 128 | bytes 1024 | tf_op jit(solution)/shard_map/psum | solution.py:68
  132.6 0.8 multiply_convert_fusion
  133.3 0.0 all-gather.5.cloned.1.call-update
  133.4 0.0 reduce-scatter.2.cloned.1.call-start
  133.4 42.0 %all-gather.5.cloned.1.call-done = bf16[5120,128]{0,1:T(8,128)(2,1)} async-done(((bf16[640,128]{0,1:T(8,128)(2,1)}), bf16[5120,128]{0,1:T(8,128)(2,1)}) %all-gather.5.cloned.1.call-update) | async-done | bytes 1310736 | tf_op jit(solution)/shard_map/all_gather | solution.py:72
  175.4 0.0 copy-start.2
  175.4 11.0 %convolution_bitcast_fusion.2 = f32[1728,128]{1,0:T(8,128)S(1)} fusion(bf16[5120,128]{0,1:T(8,128)(2,1)} %all-gather.5.cloned.1.call-done, bf16[1728,5120]{1,0:T(8,128)(2,1)} %param.17), kind=kOutput, calls=%fused_computation.3 | convolution fusion | flops 2264924160 | bytes 19890176 | tf_op jit(solution)/shard_map/dot_general | solution.py:73
  186.5 0.0 copy-done.2
  186.5 0.0 copy-start.1
  186.5 20.6 %convolution_bitcast_fusion = f32[5120,128]{0,1:T(8,128)} fusion(bf16[1728,5120]{1,0:T(8,128)(2,1)} %param.19, bf16[5120,128]{0,1:T(8,128)(2,1)S(1)} %copy-done.2, bf16[1728,5120]{1,0:T(8,128)(2,1)} %param.18, f32[1728,128]{1,0:T(8,128)S(1)} %convolution_bitcast_fusion.2), kind=kOutput, calls=%fused_computation | convolution fusion | flops 4531175424 | bytes 40206336 | tf_op jit(solution)/shard_map/dot_general | solution.py:76
  207.1 0.0 reduce-scatter.2.cloned.1.call-update
  207.2 69.8 %reduce-scatter.2.cloned.1.call-done = f32[640,128]{0,1:T(8,128)} async-done(((f32[5120,128]{0,1:T(8,128)}), f32[640,128]{0,1:T(8,128)}) %reduce-scatter.2.cloned.1.call-update) | async-done | bytes 327696 | tf_op jit(solution)/shard_map/reduce_scatter | solution.py:79
  277.0 1.0 fusion.13
  278.0 0.8 copy.40
  278.8 0.0 copy-done.1
  (8 shorter events, 0.1 us)
Async XLA Ops:
  6.5 62.6 %copy-start = (bf16[64,640]{1,0:T(8,128)(2,1)S(1)}, bf16[64,640]{1,0:T(8,128)(2,1)}, u32[]{:S(2)}) copy-start(bf16[64,640]{1,0:T(8,128)(2,1)} %param.10) | copy-start | bytes 245764
  6.5 62.3 %copy-start.5 = (s32[16]{0:T(128)S(1)}, s32[16]{0:T(128)}, u32[]{:S(2)}) copy-start(s32[16]{0:T(128)} %param.13) | copy-start | bytes 196
  6.5 103.6 %all-gather.3.cloned.1.call-start = ((), (), s32[]{:S(2)}) async-start(), calls=%async_computation.2 | async-start | bytes 4096000 | tf_op jit(solution)/shard_map/all_gather | solution.py:61
  37.0 37.4 %copy-start.3 = (bf16[1,640,128]{2,1,0:T(8,128)(2,1)S(1)}, bf16[1,640,128]{2,1,0:T(8,128)(2,1)}, u32[]{:S(2)}) copy-start(bf16[1,640,128]{2,1,0:T(8,128)(2,1)} %param.15) | copy-start | bytes 491524
  68.6 5.9 %copy-start.4 = (bf16[640]{0:T(1024)(128)(2,1)S(1)}, bf16[640]{0:T(1024)(128)(2,1)}, u32[]{:S(2)}) copy-start(bf16[640]{0:T(1024)(128)(2,1)} %param.16) | copy-start | bytes 3844
  71.0 7.5 %all-to-all-start = ((bf16[4,16,640]{2,1,0:T(8,128)(2,1)}), bf16[4,16,640]{2,1,0:T(8,128)(2,1)S(1)}, u32[]{:S(2)}, u32[]{:S(2)}) async-start(bf16[4,16,640]{2,1,0:T(8,128)(2,1)} %reshape_reshape.3), calls=%async_computation | async-start | bytes 163840 | tf_op jit(solution)/shard_map/all_to_all | solution.py:60
  74.3 101.2 %all-gather.5.cloned.1.call-start = ((), (), s32[]{:S(2)}) async-start(), calls=%async_computation.3 | async-start | bytes 1474560 | tf_op jit(solution)/shard_map/all_gather | solution.py:72
  133.4 143.6 %reduce-scatter.2.cloned.1.call-start = ((), (), s32[]{:S(2)}) async-start(), calls=%async_computation.4 | async-start | bytes 2949120 | tf_op jit(solution)/shard_map/reduce_scatter | solution.py:79
  175.4 11.1 %copy-start.2 = (bf16[5120,128]{0,1:T(8,128)(2,1)S(1)}, bf16[5120,128]{0,1:T(8,128)(2,1)}, u32[]{:S(2)}) copy-start(bf16[5120,128]{0,1:T(8,128)(2,1)} %all-gather.5.cloned.1.call-done) | copy-start | bytes 3932164
  186.5 92.3 %copy-start.1 = (bf16[64,640]{1,0:T(8,128)(2,1)S(1)}, bf16[64,640]{1,0:T(8,128)(2,1)}, u32[]{:S(2)}) copy-start(bf16[64,640]{1,0:T(8,128)(2,1)} %param.10) | copy-start | bytes 245764
Sparse Core Ops, SparseCore 0:
  8.9 30.2 all-gather.2
  133.5 41.9 all-gather.4
  207.3 69.6 reduce-scatter.1
where the time goes:
time: 289 us; the launch traced here: 285 us
  waiting for transfers between devices  116 us (40%)
  blocking collectives  112 us (39%)
  matrix products  35.1 us (12%)
  between operations  13.3 us (5%)
  starting transfers between devices  3.38 us (1%)
    reduce_scatter x1, waiting for transfers between devices, on_device(): down = lax.psum_scatter(term, 'seq', scatter_dimension=0, tiled=True)  69.8 us
    all_gather x1, waiting for transfers between devices, on_device(): piece = lax.all_gather(normed, 'seq', axis=0, tiled=True)  42 us
    all_gather x1, blocking collectives, on_device(): piece = lax.all_gather(group_rows, 'seq', axis=0, tiled=True)  31.7 us
    all_gather x1, blocking collectives, on_device(): value_piece = lax.all_gather(values, 'seq', axis=0, tiled=True)  31.6 us
    all_gather x1, blocking collectives, on_device(): key_piece = lax.all_gather(keys, 'seq', axis=0, tiled=True)  29.5 us
    dot_general x1, matrix products, on_device(): lax.dot_general(w_down, hidden, (((0,), (0,)), ((), ())), preferred_eleme...  20.6 us
    psum x1, blocking collectives, on_device(): squares = lax.psum(jnp.sum(carried * carried, axis=0), 'seq')  19.7 us
    dot_general x1, matrix products, on_device(): gate_sum = jnp.dot(w_gate, piece, preferred_element_type=jnp.float32)  11 us
  transfers between devices with their start and end apart: 4, of which 3 were waited for; matrix products, arithmetic and copies ran while one was open for 1% of the time, Pallas kernels for 0%

commit v1 on v0

--- a/solution.py
+++ b/solution.py
@@ -1,6 +1,10 @@
+import functools
+
 import jax
 import jax.numpy as jnp
 from jax import lax
+from jax.experimental import pallas as pl
+from jax.experimental.pallas import tpu as pltpu
 from jax.sharding import PartitionSpec as P
 
 D = 5120
@@ -13,6 +17,252 @@
     match = owners[:, None] == jnp.arange(order.shape[0], dtype=jnp.int32)[None, :]
     first = jnp.sum(jnp.where(match, order[None, :], 0), axis=1)
     return first * block_rows + row_ids % block_rows
+
+
+VMEM_BUDGET = 60 * 2**20
+
+
+class Copies:
+    def __init__(self, send_sems):
+        self.sems = send_sems
+        self.started = []
+
+    def send(self, src, dst, recv_sem, device):
+        copy = pltpu.make_async_remote_copy(
+            src_ref=src,
+            dst_ref=dst,
+            send_sem=self.sems.at[len(self.started)],
+            recv_sem=recv_sem,
+            device_id=device,
+            device_id_type=pl.DeviceIdType.MESH,
+        )
+        copy.start()
+        self.started.append(copy)
+
+    def arrived(self, dst, recv_sem, device):
+        pltpu.make_async_remote_copy(
+            src_ref=dst,
+            dst_ref=dst,
+            send_sem=self.sems.at[0],
+            recv_sem=recv_sem,
+            device_id=device,
+            device_id_type=pl.DeviceIdType.MESH,
+        ).wait_recv()
+
+    def finish(self):
+        for copy in self.started:
+            copy.wait_send()
+
+
+def greet(peers):
+    barrier = pltpu.get_barrier_semaphore()
+    for peer in peers:
+        pl.semaphore_signal(barrier, inc=1, device_id=peer, device_id_type=pl.DeviceIdType.MESH)
+    pl.semaphore_wait(barrier, len(peers))
+
+
+def mlp_kernel(
+    n_seq, scaled_ref, squares_ref, carried_ref, w_gate_hbm, w_up_hbm, w_down_hbm, out_ref,
+    x, sq, w_gate, w_up, w_down, gate_acc, up_acc, hidden, part, from_rep, to_y, from_y, to_z, from_z,
+    weight_sem, own_sem, send_sem, x_sem, sq_sem, rep_sem, y_sem, z_sem,
+):
+    section, s, r = lax.axis_index("section"), lax.axis_index("seq"), lax.axis_index("rep")
+    depth = n_seq // 2
+    tokens, columns = scaled_ref.shape
+    half = w_gate.shape[0]
+    z, y = s // 2, lax.rem(s, 2)
+    other_y, other_r = 1 - y, 1 - r
+
+    def at(z_step, y_index):
+        return lax.rem(z + z_step, depth) * 2 + y_index
+
+    def dev(seq_index, rep_index):
+        return (section, seq_index, rep_index)
+
+    rep_mate, y_mate = dev(s, other_r), dev(at(0, other_y), r)
+    loads = []
+    for i, (hbm, vmem) in enumerate(((w_gate_hbm, w_gate), (w_up_hbm, w_up), (w_down_hbm, w_down))):
+        load = pltpu.make_async_copy(hbm.at[pl.ds(r * half, half), :], vmem, weight_sem.at[i])
+        load.start()
+        loads.append(load)
+
+    def rows(rep_index):
+        return pl.ds(rep_index * tokens, tokens)
+
+    own = [
+        pltpu.make_async_copy(scaled_ref, x.at[s, rows(r), :], own_sem.at[0]),
+        pltpu.make_async_copy(squares_ref, sq.at[s, r], own_sem.at[1]),
+    ]
+    for copy in own:
+        copy.start()
+    peers = [
+        dev(lax.rem(s + k, n_seq), rep_index)
+        for k in range(n_seq)
+        for rep_index in (r, other_r)
+        if (k, rep_index is r) != (0, True)
+    ]
+    greet(peers)
+    copies = Copies(send_sem)
+    for peer in peers:
+        copies.send(squares_ref, sq.at[s, r], sq_sem.at[s, r], peer)
+
+    def forward(src, seq_index, device):
+        copies.send(src, x.at[seq_index, rows(r), :], x_sem.at[seq_index, r], device)
+
+    forward(scaled_ref, s, y_mate)
+    for k in range(1, depth):
+        forward(scaled_ref, s, dev(at(k, y), r))
+    forward(scaled_ref, s, rep_mate)
+    for copy in own:
+        copy.wait()
+
+    first = True
+
+    def accumulate(seq_index):
+        nonlocal first
+        copies.arrived(x.at[seq_index, rows(other_r), :], x_sem.at[seq_index, other_r], rep_mate)
+        block = x[seq_index]
+        span = pl.ds(pl.multiple_of(seq_index * columns, 128), columns)
+        for w, acc, load in ((w_gate, gate_acc, loads[0]), (w_up, up_acc, loads[1])):
+            if first:
+                load.wait()
+            term = lax.dot_general(
+                block, w[:, span], (((1,), (1,)), ((), ())), preferred_element_type=jnp.float32
+            )
+            if first:
+                acc[...] = term
+            else:
+                acc[...] += term
+        first = False
+
+    events = []
+    for k in range(depth):
+        if k:
+            events.append((k, 0))
+        if k >= 1:
+            events.append((k - 1, 1))
+    events.append((depth - 1, 1))
+    pending = s
+    for k, from_mate in events:
+        seq_index = at(depth - k, other_y if from_mate else y)
+        piece = x.at[seq_index, rows(r), :]
+        copies.arrived(piece, x_sem.at[seq_index, r], y_mate)
+        if not from_mate:
+            forward(piece, seq_index, y_mate)
+        forward(piece, seq_index, rep_mate)
+        accumulate(pending)
+        pending = seq_index
+    for k in range(n_seq):
+        for rep_index in (r, other_r):
+            if (k, rep_index is r) != (0, True):
+                seq_index = lax.rem(s + k, n_seq)
+                copies.arrived(sq.at[seq_index, rep_index], sq_sem.at[seq_index, rep_index], rep_mate)
+    accumulate(pending)
+
+    for rep_index in range(2):
+        total = jnp.sum(sq[:, rep_index], axis=0)
+        factor = lax.rsqrt(total / (n_seq * columns) + 1e-05)
+        factor = jnp.transpose(factor)[:, :1]
+        own_rows = slice(rep_index * tokens, (rep_index + 1) * tokens)
+        gate = gate_acc[own_rows, :] * factor
+        up = up_acc[own_rows, :] * factor
+        hidden[own_rows, :] = (gate / (1.0 + jnp.exp(-gate)) * up).astype(jnp.bfloat16)
+    loads[2].wait()
+
+    order = [(k % depth, 1) for k in range(1, depth + 1)] + [(k % depth, 0) for k in range(1, depth + 1)]
+    slot_of = {step: i for i, step in enumerate(order)}
+
+    def joined(slot):
+        return part[slot, rows(r), :] + from_rep[slot]
+
+    def after_rep(slot):
+        k, to_mate = order[slot]
+        copies.arrived(from_rep.at[slot], rep_sem.at[slot], rep_mate)
+        if to_mate:
+            to_y[k] = joined(slot).astype(jnp.bfloat16)
+            copies.send(to_y.at[k], from_y.at[k], y_sem.at[k], y_mate)
+
+    for slot, (k, to_mate) in enumerate(order):
+        seq_index = at(k, other_y if to_mate else y)
+        span = pl.ds(pl.multiple_of(seq_index * columns, 128), columns)
+        part[slot] = jnp.dot(hidden[...], w_down[:, span], preferred_element_type=jnp.float32)
+        copies.send(part.at[slot, rows(other_r), :], from_rep.at[slot], rep_sem.at[slot], rep_mate)
+        if slot:
+            after_rep(slot - 1)
+    after_rep(len(order) - 1)
+    for k in range(1, depth):
+        copies.arrived(from_y.at[k], y_sem.at[k], y_mate)
+        to_z[k - 1] = (joined(slot_of[k, 0]) + from_y[k].astype(jnp.float32)).astype(jnp.bfloat16)
+        copies.send(to_z.at[k - 1], from_z.at[k - 1], z_sem.at[k - 1], dev(at(k, y), r))
+    copies.arrived(from_y.at[0], y_sem.at[0], y_mate)
+    total = carried_ref[...] + joined(slot_of[0, 0]) + from_y[0].astype(jnp.float32)
+    for k in range(1, depth):
+        copies.arrived(from_z.at[k - 1], z_sem.at[k - 1], y_mate)
+        total += from_z[k - 1].astype(jnp.float32)
+    out_ref[...] = total.astype(jnp.bfloat16)
+    copies.finish()
+
+
+def mlp(scaled, squares, carried, w_gate, w_up, w_down):
+    n_seq, n_rep = lax.axis_size("seq"), lax.axis_size("rep")
+    tokens, columns = scaled.shape
+    features = w_gate.shape[1]
+    half = w_gate.shape[0] // n_rep
+    depth = n_seq // 2
+    sends = n_seq * n_rep + (depth + 1) + 2 * n_seq + 2 * n_seq + 2 * depth
+    f32, bf16 = jnp.float32, jnp.bfloat16
+    vmem = pl.BlockSpec(memory_space=pltpu.VMEM)
+    hbm = pl.BlockSpec(memory_space=pl.ANY)
+    dma = pltpu.SemaphoreType.DMA
+    return pl.pallas_call(
+        functools.partial(mlp_kernel, n_seq),
+        out_shape=jax.ShapeDtypeStruct((tokens, columns), bf16),
+        in_specs=[vmem, vmem, vmem, hbm, hbm, hbm],
+        out_specs=vmem,
+        scratch_shapes=[
+            pltpu.VMEM((n_seq, n_rep * tokens, columns), bf16),
+            pltpu.VMEM((n_seq, n_rep, 8, tokens), f32),
+            pltpu.VMEM((half, features), bf16),
+            pltpu.VMEM((half, features), bf16),
+            pltpu.VMEM((half, features), bf16),
+            pltpu.VMEM((n_rep * tokens, half), f32),
+            pltpu.VMEM((n_rep * tokens, half), f32),
+            pltpu.VMEM((n_rep * tokens, half), bf16),
+            pltpu.VMEM((n_seq, n_rep * tokens, columns), f32),
+            pltpu.VMEM((n_seq, tokens, columns), f32),
+            pltpu.VMEM((depth, tokens, columns), bf16),
+            pltpu.VMEM((depth, tokens, columns), bf16),
+            pltpu.VMEM((depth - 1, tokens, columns), bf16),
+            pltpu.VMEM((depth - 1, tokens, columns), bf16),
+            dma((3,)),
+            dma((2,)),
+            dma((sends,)),
+            dma((n_seq, n_rep)),
+            dma((n_seq, n_rep)),
+            dma((n_seq,)),
+            dma((depth,)),
+            dma((depth - 1,)),
+        ],
+        compiler_params=pltpu.CompilerParams(
+            collective_id=1, has_side_effects=True, vmem_limit_bytes=VMEM_BUDGET
+        ),
+    )(scaled, squares, carried, w_gate, w_up, w_down)
+
+
+def kernels_fit(wo, w_gate, tokens):
+    n_seq, n_rep = lax.axis_size("seq"), lax.axis_size("rep")
+    columns = wo.shape[1]
+    half = w_gate.shape[0] // n_rep
+    held = 3 * half * w_gate.shape[1] * 2 + n_seq * tokens * columns * 16 + 20 * tokens * half
+    return (
+        n_rep == 2
+        and n_seq % 2 == 0
+        and n_seq >= 4
+        and columns % 128 == 0
+        and tokens % 128 == 0
+        and w_gate.shape[0] % (16 * n_rep) == 0
+        and held < VMEM_BUDGET - 8 * 2**20
+    )
 
 
 def on_device(queries, keys, values, block_order, wo, resid, gain, w_gate, w_up, w_down):
@@ -63,6 +313,13 @@
     flat = piece.reshape(piece.shape[0] * piece.shape[1], piece.shape[2])
     product = jnp.dot(flat, wo_columns, preferred_element_type=jnp.float32)
     projected = product.reshape(piece.shape[0], piece.shape[1], columns)
+    if kernels_fit(wo, w_gate, token_count):
+        base = resid.reshape(columns, token_count).T.astype(jnp.float32)
+        carried = base + projected.reshape(token_count, columns)
+        squares = jnp.broadcast_to(jnp.sum(carried * carried, axis=1)[None, :], (8, token_count))
+        scaled = (carried * gain.astype(jnp.float32)[None, :]).astype(jnp.bfloat16)
+        mixed = mlp(scaled, squares, carried, w_gate, w_up, w_down)
+        return mixed.T.reshape(resid.shape)
     projected_cols = projected.reshape(token_count, columns).T
     carried = resid.reshape(columns, token_count).astype(jnp.float32) + projected_cols
     squares = lax.psum(jnp.sum(carried * carried, axis=0), "seq")

time: 289 us -> 181 us (0.63); the launches traced: 285 us -> 180 us
  waiting for transfers between devices: 116 us -> 4.69 us
  Pallas kernels: 0 us -> 57.8 us
  matrix products: 35.1 us -> 4.12 us
  blocking collectives: 112 us -> 92.7 us
    reduce_scatter x1 -> x0, waiting for transfers between devices: 69.8 us -> none  [on_device(): down = lax.psum_scatter(term, 'seq', scatter_dimension=0, tiled=True)]
    pallas_call x0 -> x1, Pallas kernels: none -> 57.8 us  [mlp(): pl.pallas_call(functools.partial(mlp_kernel, n_seq), out_shape=jax.ShapeD...]
    all_gather x1 -> x0, waiting for transfers between devices: 42 us -> none  [on_device(): piece = lax.all_gather(normed, 'seq', axis=0, tiled=True)]
    dot_general x2 -> x0, matrix products: 31.7 us -> none  [the longest x1 20.6 us: on_device(): lax.dot_general(w_down, hidden, (((0,), (0,)), ((), ())), preferred_eleme...]
    psum x1 -> x0, blocking collectives: 19.7 us -> none  [on_device(): squares = lax.psum(jnp.sum(carried * carried, axis=0), 'seq')]
  transfers between devices with their start and end apart: 4 -> 2, of which waited for: 3 -> 1; matrix products, arithmetic and copies ran while one was open for 1% -> 2% of each run, Pallas kernels for 0% -> 0%
where the time goes in v1:
time: 181 us; the launch traced here: 180 us
  blocking collectives  92.7 us (51%)
  Pallas kernels  57.8 us (32%)
  between operations  13.5 us (7%)
  waiting for transfers between devices  4.69 us (3%)
  matrix products  4.12 us (2%)
  local copies, waits for them, and re-layouts  3.81 us (2%)
  starting transfers between devices  3.3 us (2%)
    pallas_call x1, Pallas kernels, mlp(): pl.pallas_call(functools.partial(mlp_kernel, n_seq), out_shape=jax.ShapeD...  57.8 us
    all_gather x1, blocking collectives, on_device(): piece = lax.all_gather(group_rows, 'seq', axis=0, tiled=True)  31.7 us
    all_gather x1, blocking collectives, on_device(): value_piece = lax.all_gather(values, 'seq', axis=0, tiled=True)  31.6 us
    all_gather x1, blocking collectives, on_device(): key_piece = lax.all_gather(keys, 'seq', axis=0, tiled=True)  29.5 us
    all_to_all x1, waiting for transfers between devices, on_device(): lax.all_to_all(parts, ('section', 'rep'), split_axis=0, concat_axis=2, ti...  3.98 us
  transfers between devices with their start and end apart: 2, of which 1 were waited for; matrix products, arithmetic and copies ran while one was open for 2% of the time, Pallas kernels for 0%

profile of v1, /device:TPU:24, one launch (start us, length us, event | category | flops | bytes accessed | tf_op | source)
XLA Modules:
  0.0 180.5 jit_solution(7464097897790803104)
XLA Ops:
  6.5 0.0 copy-start
  6.5 0.0 copy-start.3
  6.5 0.0 all-gather.2.cloned.1.call-start
  6.5 0.7 all-gather.2.cloned.1.call-update
  7.3 29.5 %all_gather.12 = bf16[512,640]{1,0:T(8,128)(2,1)S(1)} all-gather(bf16[64,640]{1,0:T(8,128)(2,1)} %param.11), channel_id=1, replica_groups=mesh['section'=2,'seq'=8,'rep'=2] {'seq'}, dimensions={0}, use_global_device_ids=true | all-gather | bytes 737280 | tf_op jit(solution)/shard_map/all_gather | solution.py:280
  36.7 0.3 copy.33
  37.0 0.0 copy-start.1
  37.0 31.6 %all_gather.13 = bf16[512,640]{1,0:T(8,128)(2,1)S(1)} all-gather(bf16[64,640]{1,0:T(8,128)(2,1)} %param.12), channel_id=1, replica_groups=mesh['section'=2,'seq'=8,'rep'=2] {'seq'}, dimensions={0}, use_global_device_ids=true | all-gather | bytes 737280 | tf_op jit(solution)/shard_map/all_gather | solution.py:281
  68.6 0.0 copy-start.2
  68.6 0.3 copy.36
  68.9 0.0 copy-done.3
  68.9 0.1 select_reduce_fusion.2
  69.0 0.1 select_reduce_fusion.1
  69.1 0.1 broadcast_compare_fusion
  69.2 0.0 copy-done
  69.2 0.3 select_reduce_fusion
  69.5 0.3 fusion.3
  69.8 0.4 fusion.2
  70.2 0.1 copy.38
  70.2 0.7 reshape_reshape.3
  71.0 3.3 %all-to-all-start = ((bf16[4,16,640]{2,1,0:T(8,128)(2,1)}), bf16[4,16,640]{2,1,0:T(8,128)(2,1)S(1)}, u32[]{:S(2)}, u32[]{:S(2)}) async-start(bf16[4,16,640]{2,1,0:T(8,128)(2,1)} %reshape_reshape.3), calls=%async_computation | async-start | bytes 163840 | tf_op jit(solution)/shard_map/all_to_all | solution.py:310
  74.3 0.0 copy-done.1
  74.3 0.2 copy.32
  74.5 0.0 copy-done.2
  74.5 4.0 %all-to-all-done = bf16[4,16,640]{2,1,0:T(8,128)(2,1)S(1)} async-done(((bf16[4,16,640]{2,1,0:T(8,128)(2,1)}), bf16[4,16,640]{2,1,0:T(8,128)(2,1)S(1)}, u32[]{:S(2)}, u32[]{:S(2)}) %all-to-all-start) | async-done | bytes 81952 | tf_op jit(solution)/shard_map/all_to_all | solution.py:310
  78.5 31.7 %all_gather.14 = bf16[8,16,2560]{2,1,0:T(8,128)(2,1)S(1)} all-gather(bf16[1,16,2560]{2,1,0:T(8,128)(2,1)S(1)} %bitcast.44), channel_id=1, replica_groups=mesh['section'=2,'seq'=8,'rep'=2] {'seq'}, dimensions={0}, use_global_device_ids=true | all-gather | bytes 737280 | tf_op jit(solution)/shard_map/all_gather | solution.py:312
  110.1 0.0 all-gather.2.cloned.1.call-done
  110.1 3.4 %multiply_reduce_fusion = (f32[128]{0:T(128)S(1)}, bf16[128,640]{1,0:T(8,128)(2,1)}, f32[128,640]{1,0:T(8,128)}) fusion(f32[640]{0:T(1024)S(1)} %convert_element_type.26, bf16[128,2560]{1,0:T(8,128)(2,1)S(1)} %bitcast.40, bf16[2560,640]{1,0:T(8,128)(2,1)} %all-gather.2.cloned.1.call-done, bf16[1,640,128]{1,2,0:T(8,128)(2,1)S(1)} %copy.32), kind=kOutput, calls=%fused_computation.11 | convolution fusion | flops 419921792 | bytes 4590592 | tf_op jit(solution)/shard_map/dot_general | solution.py:314
  113.5 0.6 broadcast_in_dim.71.squares_ref
  114.1 57.8 %shard_map.100 = bf16[128,640]{1,0:T(8,128)(2,1)} custom-call(bf16[128,640]{1,0:T(8,128)(2,1)} %get-tuple-element.6.scaled_ref, f32[8,128]{1,0:T(8,128)} %broadcast_in_dim.71.squares_ref, f32[128,640]{1,0:T(8,128)} %get-tuple-element.9.carried_ref, bf16[1728,5120]{1,0:T(8,128)(2,1)} %w_gate_hbm.1, bf16[1728,5120]{1,0:T(8,128)(2,1)} %w_up_hbm.1, ...), custom_call_target="tpu_custom_call" | custom-call | tf_op jit(solution)/shard_map/pallas_call | solution.py:217
  171.9 1.7 copy.40
  (7 shorter events, 0.0 us)
Async XLA Ops:
  6.5 62.6 %copy-start = (bf16[64,640]{1,0:T(8,128)(2,1)S(1)}, bf16[64,640]{1,0:T(8,128)(2,1)}, u32[]{:S(2)}) copy-start(bf16[64,640]{1,0:T(8,128)(2,1)} %param.10) | copy-start | bytes 245764
  6.5 62.3 %copy-start.3 = (s32[16]{0:T(128)S(1)}, s32[16]{0:T(128)}, u32[]{:S(2)}) copy-start(s32[16]{0:T(128)} %param.13) | copy-start | bytes 196
  6.5 103.6 %all-gather.2.cloned.1.call-start = ((), (), s32[]{:S(2)}) async-start(), calls=%async_computation.1 | async-start | bytes 4096000 | tf_op jit(solution)/shard_map/all_gather | solution.py:311
  37.0 37.3 %copy-start.1 = (bf16[1,640,128]{2,1,0:T(8,128)(2,1)S(1)}, bf16[1,640,128]{2,1,0:T(8,128)(2,1)}, u32[]{:S(2)}) copy-start(bf16[1,640,128]{2,1,0:T(8,128)(2,1)} %param.15) | copy-start | bytes 491524
  68.6 5.9 %copy-start.2 = (bf16[640]{0:T(1024)(128)(2,1)S(1)}, bf16[640]{0:T(1024)(128)(2,1)}, u32[]{:S(2)}) copy-start(bf16[640]{0:T(1024)(128)(2,1)} %param.16) | copy-start | bytes 3844
  71.0 7.5 %all-to-all-start = ((bf16[4,16,640]{2,1,0:T(8,128)(2,1)}), bf16[4,16,640]{2,1,0:T(8,128)(2,1)S(1)}, u32[]{:S(2)}, u32[]{:S(2)}) async-start(bf16[4,16,640]{2,1,0:T(8,128)(2,1)} %reshape_reshape.3), calls=%async_computation | async-start | bytes 163840 | tf_op jit(solution)/shard_map/all_to_all | solution.py:310
Sparse Core Ops, SparseCore 0:
  8.9 30.2 all-gather.1

commit v2 on v1

--- a/solution.py
+++ b/solution.py
@@ -61,23 +61,32 @@
     pl.semaphore_wait(barrier, len(peers))
 
 
-def mlp_kernel(
-    n_seq, scaled_ref, squares_ref, carried_ref, w_gate_hbm, w_up_hbm, w_down_hbm, out_ref,
+def layer_kernel(
+    n_seq, n_rep, groups,
+    q_ref, k_ref, v_ref, bias_ref, wo_ref, base_ref, gain_ref, w_gate_hbm, w_up_hbm, w_down_hbm, out_ref,
+    keys, values, attended, proj, proj_low, from_group, carried,
     x, sq, w_gate, w_up, w_down, gate_acc, up_acc, hidden, part, from_rep, to_y, from_y, to_z, from_z,
-    weight_sem, own_sem, send_sem, x_sem, sq_sem, rep_sem, y_sem, z_sem,
+    weight_sem, own_sem, send_sem, k_sem, v_sem, att_sem, group_sem, x_sem, sq_sem, rep_sem, y_sem, z_sem,
 ):
     section, s, r = lax.axis_index("section"), lax.axis_index("seq"), lax.axis_index("rep")
     depth = n_seq // 2
-    tokens, columns = scaled_ref.shape
+    tokens, columns = base_ref.shape
+    seq_dev = q_ref.shape[0]
+    sub = seq_dev // groups
     half = w_gate.shape[0]
     z, y = s // 2, lax.rem(s, 2)
     other_y, other_r = 1 - y, 1 - r
+    group = section * n_rep + r
 
     def at(z_step, y_index):
         return lax.rem(z + z_step, depth) * 2 + y_index
 
     def dev(seq_index, rep_index):
         return (section, seq_index, rep_index)
+
+    def group_dev(step):
+        other = lax.rem(group + step, groups)
+        return (other // n_rep, s, lax.rem(other, n_rep))
 
     rep_mate, y_mate = dev(s, other_r), dev(at(0, other_y), r)
     loads = []
@@ -90,8 +99,8 @@
         return pl.ds(rep_index * tokens, tokens)
 
     own = [
-        pltpu.make_async_copy(scaled_ref, x.at[s, rows(r), :], own_sem.at[0]),
-        pltpu.make_async_copy(squares_ref, sq.at[s, r], own_sem.at[1]),
+        pltpu.make_async_copy(k_ref, keys.at[s], own_sem.at[0]),
+        pltpu.make_async_copy(v_ref, values.at[s], own_sem.at[1]),
     ]
     for copy in own:
         copy.start()
@@ -101,20 +110,101 @@
         for rep_index in (r, other_r)
         if (k, rep_index is r) != (0, True)
     ]
-    greet(peers)
+    greet(peers + [(lax.rem(section + k, groups // n_rep), s, i) for k in range(1, groups // n_rep) for i in range(n_rep)])
     copies = Copies(send_sem)
-    for peer in peers:
-        copies.send(squares_ref, sq.at[s, r], sq_sem.at[s, r], peer)
-
-    def forward(src, seq_index, device):
-        copies.send(src, x.at[seq_index, rows(r), :], x_sem.at[seq_index, r], device)
-
-    forward(scaled_ref, s, y_mate)
+
+    def spread(src, dst, sem):
+        copies.send(src, dst.at[s], sem.at[s], y_mate)
+        for k in range(1, depth):
+            copies.send(src, dst.at[s], sem.at[s], dev(at(k, y), r))
+
+    def take(dst, sem, k, from_mate):
+        seq_index = at(depth - k, other_y if from_mate else y)
+        copies.arrived(dst.at[seq_index], sem.at[seq_index], y_mate)
+        if not from_mate:
+            copies.send(dst.at[seq_index], dst.at[seq_index], sem.at[seq_index], y_mate)
+        return seq_index
+
+    events = []
+    for k in range(depth):
+        if k:
+            events.append((k, 0))
+            events.append((k - 1, 1))
+    events.append((depth - 1, 1))
+
+    spread(k_ref, keys, k_sem)
+    spread(v_ref, values, v_sem)
     for k in range(1, depth):
-        forward(scaled_ref, s, dev(at(k, y), r))
-    forward(scaled_ref, s, rep_mate)
+        take(keys, k_sem, k, 0)
+    for k in range(1, depth):
+        take(values, v_sem, k, 0)
     for copy in own:
         copy.wait()
+    for k in range(depth):
+        take(keys, k_sem, k, 1)
+    heads = q_ref.shape[1] // HEAD_DIM
+    all_keys = keys.reshape(n_seq * seq_dev, q_ref.shape[1])
+    all_values = values.reshape(n_seq * seq_dev, q_ref.shape[1])
+    probs, totals = [], []
+    for h in range(heads):
+        span = slice(h * HEAD_DIM, (h + 1) * HEAD_DIM)
+        scores = lax.dot_general(
+            q_ref[:, span], all_keys[:, span], (((1,), (1,)), ((), ())), preferred_element_type=jnp.float32
+        )
+        scores = scores * HEAD_DIM**-0.5 + bias_ref[...]
+        prob = jnp.exp(scores - jnp.max(scores, axis=1, keepdims=True))
+        totals.append(jnp.sum(prob, axis=1, keepdims=True))
+        probs.append(prob.astype(jnp.bfloat16))
+    for k in range(depth):
+        take(values, v_sem, k, 1)
+    for h in range(heads):
+        span = slice(h * HEAD_DIM, (h + 1) * HEAD_DIM)
+        weighted = jnp.dot(probs[h], all_values[:, span], preferred_element_type=jnp.float32)
+        attended[s, :, span] = (weighted / totals[h]).astype(jnp.bfloat16)
+    spread(attended.at[s], attended, att_sem)
+
+    def project(seq_index):
+        proj[...] = jnp.dot(attended[seq_index], wo_ref[...], preferred_element_type=jnp.float32)
+        proj_low[seq_index] = proj[...].astype(jnp.bfloat16)
+        spot = pl.ds(pl.multiple_of(seq_index * sub, sub), sub)
+        carried[spot, :] = base_ref[spot, :] + proj[pl.ds(pl.multiple_of(group * sub, sub), sub), :]
+        for step in range(1, groups):
+            other = lax.rem(group + step, groups)
+            copies.send(
+                proj_low.at[seq_index, pl.ds(pl.multiple_of(other * sub, sub), sub), :],
+                from_group.at[step - 1, spot, :],
+                group_sem.at[step - 1, seq_index],
+                group_dev(step),
+            )
+
+    pending = s
+    for k, from_mate in events:
+        seq_index = take(attended, att_sem, k, from_mate)
+        project(pending)
+        pending = seq_index
+    project(pending)
+    for step in range(1, groups):
+        for k in range(n_seq):
+            spot = pl.ds(k * sub, sub)
+            copies.arrived(from_group.at[step - 1, spot, :], group_sem.at[step - 1, k], rep_mate)
+    total = carried[...]
+    for step in range(1, groups):
+        total += from_group[step - 1].astype(jnp.float32)
+    carried[...] = total
+    squares = jnp.sum(total * total, axis=1, keepdims=True)
+    sq[s, r] = jnp.transpose(jnp.broadcast_to(squares, (tokens, tokens)))[:8]
+    x[s, rows(r), :] = (total * gain_ref[...]).astype(jnp.bfloat16)
+    for peer in peers:
+        copies.send(sq.at[s, r], sq.at[s, r], sq_sem.at[s, r], peer)
+
+    def forward(seq_index, device):
+        piece = x.at[seq_index, rows(r), :]
+        copies.send(piece, piece, x_sem.at[seq_index, r], device)
+
+    forward(s, y_mate)
+    for k in range(1, depth):
+        forward(s, dev(at(k, y), r))
+    forward(s, rep_mate)
 
     first = True
 
@@ -135,21 +225,14 @@
                 acc[...] += term
         first = False
 
-    events = []
-    for k in range(depth):
-        if k:
-            events.append((k, 0))
-        if k >= 1:
-            events.append((k - 1, 1))
-    events.append((depth - 1, 1))
     pending = s
     for k, from_mate in events:
         seq_index = at(depth - k, other_y if from_mate else y)
         piece = x.at[seq_index, rows(r), :]
         copies.arrived(piece, x_sem.at[seq_index, r], y_mate)
         if not from_mate:
-            forward(piece, seq_index, y_mate)
-        forward(piece, seq_index, rep_mate)
+            forward(seq_index, y_mate)
+        forward(seq_index, rep_mate)
         accumulate(pending)
         pending = seq_index
     for k in range(n_seq):
@@ -195,7 +278,7 @@
         to_z[k - 1] = (joined(slot_of[k, 0]) + from_y[k].astype(jnp.float32)).astype(jnp.bfloat16)
         copies.send(to_z.at[k - 1], from_z.at[k - 1], z_sem.at[k - 1], dev(at(k, y), r))
     copies.arrived(from_y.at[0], y_sem.at[0], y_mate)
-    total = carried_ref[...] + joined(slot_of[0, 0]) + from_y[0].astype(jnp.float32)
+    total = carried[...] + joined(slot_of[0, 0]) + from_y[0].astype(jnp.float32)
     for k in range(1, depth):
         copies.arrived(from_z.at[k - 1], z_sem.at[k - 1], y_mate)
         total += from_z[k - 1].astype(jnp.float32)
@@ -203,23 +286,32 @@
     copies.finish()
 
 
-def mlp(scaled, squares, carried, w_gate, w_up, w_down):
+def layer(q, k, v, bias, wo, base, gain, w_gate, w_up, w_down):
     n_seq, n_rep = lax.axis_size("seq"), lax.axis_size("rep")
-    tokens, columns = scaled.shape
+    groups = n_rep * lax.axis_size("section")
+    seq_dev, width = q.shape
+    tokens, columns = base.shape
     features = w_gate.shape[1]
     half = w_gate.shape[0] // n_rep
     depth = n_seq // 2
-    sends = n_seq * n_rep + (depth + 1) + 2 * n_seq + 2 * n_seq + 2 * depth
+    sends = 3 * (n_seq - 1) + n_seq * (groups - 1) + (2 * n_seq - 1) * 2 + 2 * n_seq
     f32, bf16 = jnp.float32, jnp.bfloat16
     vmem = pl.BlockSpec(memory_space=pltpu.VMEM)
     hbm = pl.BlockSpec(memory_space=pl.ANY)
     dma = pltpu.SemaphoreType.DMA
     return pl.pallas_call(
-        functools.partial(mlp_kernel, n_seq),
+        functools.partial(layer_kernel, n_seq, n_rep, groups),
         out_shape=jax.ShapeDtypeStruct((tokens, columns), bf16),
-        in_specs=[vmem, vmem, vmem, hbm, hbm, hbm],
+        in_specs=[vmem] * 7 + [hbm] * 3,
         out_specs=vmem,
         scratch_shapes=[
+            pltpu.VMEM((n_seq, seq_dev, width), bf16),
+            pltpu.VMEM((n_seq, seq_dev, width), bf16),
+            pltpu.VMEM((n_seq, seq_dev, width), bf16),
+            pltpu.VMEM((seq_dev, columns), f32),
+            pltpu.VMEM((n_seq, seq_dev, columns), bf16),
+            pltpu.VMEM((groups - 1, tokens, columns), bf16),
+            pltpu.VMEM((tokens, columns), f32),
             pltpu.VMEM((n_seq, n_rep * tokens, columns), bf16),
             pltpu.VMEM((n_seq, n_rep, 8, tokens), f32),
             pltpu.VMEM((half, features), bf16),
@@ -237,6 +329,10 @@
             dma((3,)),
             dma((2,)),
             dma((sends,)),
+            dma((n_seq,)),
+            dma((n_seq,)),
+            dma((n_seq,)),
+            dma((groups - 1, n_seq)),
             dma((n_seq, n_rep)),
             dma((n_seq, n_rep)),
             dma((n_seq,)),
@@ -246,21 +342,24 @@
         compiler_params=pltpu.CompilerParams(
             collective_id=1, has_side_effects=True, vmem_limit_bytes=VMEM_BUDGET
         ),
-    )(scaled, squares, carried, w_gate, w_up, w_down)
-
-
-def kernels_fit(wo, w_gate, tokens):
+    )(q, k, v, bias, wo, base, gain, w_gate, w_up, w_down)
+
+
+def kernels_fit(queries, wo, w_gate):
     n_seq, n_rep = lax.axis_size("seq"), lax.axis_size("rep")
     columns = wo.shape[1]
+    sub = queries.shape[0] // (n_rep * lax.axis_size("section"))
+    tokens = n_seq * sub
     half = w_gate.shape[0] // n_rep
-    held = 3 * half * w_gate.shape[1] * 2 + n_seq * tokens * columns * 16 + 20 * tokens * half
+    held = 3 * half * w_gate.shape[1] * 2 + n_seq * tokens * columns * 18 + 20 * tokens * half
     return (
         n_rep == 2
         and n_seq % 2 == 0
         and n_seq >= 4
         and columns % 128 == 0
         and tokens % 128 == 0
-        and w_gate.shape[0] % (16 * n_rep) == 0
+        and sub % 16 == 0
+        and half % 16 == 0
         and held < VMEM_BUDGET - 8 * 2**20
     )
 
@@ -274,6 +373,13 @@
     block_rows = seq_dev // 2
     query_start = lax.axis_index("seq") * seq_dev
     query_pos = key_positions(block_order, query_start, seq_dev, block_rows)
+    if kernels_fit(queries, wo, w_gate):
+        key_pos = key_positions(block_order, jnp.int32(0), n_seq * seq_dev, block_rows)
+        bias = jnp.where(key_pos[None, :] <= query_pos[:, None], 0.0, -1e30).astype(jnp.float32)
+        base = resid.reshape(wo.shape[1], n_seq * sub_rows).T.astype(jnp.float32)
+        gain_row = gain.astype(jnp.float32)[None, :]
+        mixed = layer(queries, keys, values, bias, wo, base, gain_row, w_gate, w_up, w_down)
+        return mixed.T.reshape(resid.shape)
     query_heads = queries.reshape(seq_dev, heads_dev, HEAD_DIM)
     scale = HEAD_DIM ** (-0.5)
     running_max = jnp.full((seq_dev, heads_dev), -1e30, jnp.float32)
@@ -313,13 +419,6 @@
     flat = piece.reshape(piece.shape[0] * piece.shape[1], piece.shape[2])
     product = jnp.dot(flat, wo_columns, preferred_element_type=jnp.float32)
     projected = product.reshape(piece.shape[0], piece.shape[1], columns)
-    if kernels_fit(wo, w_gate, token_count):
-        base = resid.reshape(columns, token_count).T.astype(jnp.float32)
-        carried = base + projected.reshape(token_count, columns)
-        squares = jnp.broadcast_to(jnp.sum(carried * carried, axis=1)[None, :], (8, token_count))
-        scaled = (carried * gain.astype(jnp.float32)[None, :]).astype(jnp.bfloat16)
-        mixed = mlp(scaled, squares, carried, w_gate, w_up, w_down)
-        return mixed.T.reshape(resid.shape)
     projected_cols = projected.reshape(token_count, columns).T
     carried = resid.reshape(columns, token_count).astype(jnp.float32) + projected_cols
     squares = lax.psum(jnp.sum(carried * carried, axis=0), "seq")

time: 181 us -> 104 us (0.57)
  blocking collectives: 92.7 us -> 0 us
  Pallas kernels: 57.8 us -> 96.4 us
  between operations: 13.5 us -> 0.01 us
  waiting for transfers between devices: 4.69 us -> 0 us
  matrix products: 4.12 us -> 0 us
  starting transfers between devices: 3.3 us -> 0 us
  other arithmetic: 0.55 us -> 2.99 us
    all_gather x3 -> x0, blocking collectives: 92.7 us -> none  [the longest x1 31.7 us: on_device(): piece = lax.all_gather(group_rows, 'seq', axis=0, tiled=True)]
    pallas_call x1, Pallas kernels: 57.8 us -> 96.4 us  [layer(): pl.pallas_call(functools.partial(layer_kernel, n_seq, n_rep, groups), out...]
    dot_general x3 -> x0, matrix products: 4.12 us -> none  [the longest x1 3.4 us: on_device(): product = jnp.dot(flat, wo_columns, preferred_element_type=jnp.float32)]
    all_to_all x1 -> x0, waiting for transfers between devices: 3.98 us -> none  [on_device(): lax.all_to_all(parts, ('section', 'rep'), split_axis=0, concat_axis=2, ti...]
    all_to_all x1 -> x0, starting transfers between devices: 3.29 us -> none  [on_device(): lax.all_to_all(parts, ('section', 'rep'), split_axis=0, concat_axis=2, ti...]
  transfers between devices with their start and end apart: 2 -> 0, of which waited for: 1 -> 0; matrix products, arithmetic and copies ran while one was open for 2% -> 0% of each run, Pallas kernels for 0% -> 0%
where the time goes in v2:
time: 104 us
  Pallas kernels  96.4 us (93%)
  local copies, waits for them, and re-layouts  4.06 us (4%)
  other arithmetic  2.99 us (3%)
    pallas_call x1, Pallas kernels, layer(): pl.pallas_call(functools.partial(layer_kernel, n_seq, n_rep, groups), out...  96.4 us

profile of v2, /device:TPU:24, one launch (start us, length us, event | category | flops | bytes accessed | tf_op | source)
XLA Modules:
  0.0 103.5 jit_solution(15024117858546623541)
XLA Ops:
  0.0 0.7 select_reduce_fusion.1
  0.8 0.7 select_reduce_fusion
  1.5 1.3 %reshape.70.gain_ref = f32[1,640]{1,0:T(1,128)} reshape(bf16[640]{0:T(1024)(128)(2,1)} %param.16) | data formatting | bytes 3840 | tf_op jit(solution)/shard_map/broadcast_in_dim | solution.py:380
  2.8 0.7 compare_select_fusion.bias_ref
  3.5 1.1 %copy.13 = bf16[1,640,128]{1,2,0:T(8,128)(2,1)S(1)} copy(bf16[1,640,128]{2,1,0:T(8,128)(2,1)} %param.15) | data formatting | bytes 327680 | tf_op args[5]
  4.6 0.7 convert_bitcast_fusion.base_ref
  5.3 96.4 %shard_map.100 = bf16[128,640]{1,0:T(8,128)(2,1)} custom-call(bf16[64,640]{1,0:T(8,128)(2,1)} %q_ref.1, bf16[64,640]{1,0:T(8,128)(2,1)} %k_ref.1, bf16[64,640]{1,0:T(8,128)(2,1)} %v_ref.1, f32[64,512]{1,0:T(8,128)} %compare_select_fusion.bias_ref, bf16[640,640]{1,0:T(8,128)(2,1)} %wo_ref.1, f32[128,640]{1,0:T(8,128)} %convert_bitcast_fusion.base_ref, ...), custom_call_target="tpu_custom_call" | custom-call | tf_op jit(solution)/shard_map/pallas_call | solution.py:302
  101.8 1.7 %copy.14 = bf16[1,640,128]{2,1,0:T(8,128)(2,1)} copy(bf16[1,640,128]{1,2,0:T(8,128)(2,1)} %bitcast.8) | data formatting | bytes 327680 | tf_op jit(solution)/shard_map/reshape | solution.py:382
  (4 shorter events, 0.0 us)

commit v3 on v2

--- a/solution.py
+++ b/solution.py
@@ -27,7 +27,7 @@
         self.sems = send_sems
         self.started = []
 
-    def send(self, src, dst, recv_sem, device):
+    def send(self, src, dst, recv_sem, device, when=None):
         copy = pltpu.make_async_remote_copy(
             src_ref=src,
             dst_ref=dst,
@@ -36,8 +36,11 @@
             device_id=device,
             device_id_type=pl.DeviceIdType.MESH,
         )
-        copy.start()
-        self.started.append(copy)
+        if when is None:
+            copy.start()
+        else:
+            pl.when(when)(copy.start)
+        self.started.append((copy, when))
 
     def arrived(self, dst, recv_sem, device):
         pltpu.make_async_remote_copy(
@@ -50,8 +53,11 @@
         ).wait_recv()
 
     def finish(self):
-        for copy in self.started:
-            copy.wait_send()
+        for copy, when in self.started:
+            if when is None:
+                copy.wait_send()
+            else:
+                pl.when(when)(copy.wait_send)
 
 
 def greet(peers):
@@ -61,17 +67,30 @@
     pl.semaphore_wait(barrier, len(peers))
 
 
+def mask_bias(order_ref, s, rows, count, block_rows):
+    row = lax.broadcasted_iota(jnp.int32, (rows, count), 0)
+    column = lax.broadcasted_iota(jnp.int32, (1, count), 1)
+    second = row >= block_rows
+    row_pos = jnp.where(second, order_ref[2 * s + 1], order_ref[2 * s]) * block_rows
+    row_pos += jnp.where(second, row - block_rows, row)
+    column_pos = jnp.zeros((1, count), jnp.int32)
+    for b in range(count // block_rows):
+        column_pos = jnp.where(column >= b * block_rows, (order_ref[b] - b) * block_rows + column, column_pos)
+    return jnp.where(column_pos <= row_pos, 0.0, -1e30).astype(jnp.float32)
+
+
 def layer_kernel(
     n_seq, n_rep, groups,
-    q_ref, k_ref, v_ref, bias_ref, wo_ref, base_ref, gain_ref, w_gate_hbm, w_up_hbm, w_down_hbm, out_ref,
-    keys, values, attended, proj, proj_low, from_group, carried,
+    order_ref, q_ref, k_ref, v_ref, wo_ref, resid_ref, gain_ref, w_gate_hbm, w_up_hbm, w_down_hbm, out_ref,
+    keys, values, attended, bias, proj, proj_low, from_group, carried,
     x, sq, w_gate, w_up, w_down, gate_acc, up_acc, hidden, part, from_rep, to_y, from_y, to_z, from_z,
     weight_sem, own_sem, send_sem, k_sem, v_sem, att_sem, group_sem, x_sem, sq_sem, rep_sem, y_sem, z_sem,
 ):
     section, s, r = lax.axis_index("section"), lax.axis_index("seq"), lax.axis_index("rep")
     depth = n_seq // 2
-    tokens, columns = base_ref.shape
+    columns, tokens = resid_ref.shape
     seq_dev = q_ref.shape[0]
+    block_rows = seq_dev // 2
     sub = seq_dev // groups
     half = w_gate.shape[0]
     z, y = s // 2, lax.rem(s, 2)
@@ -83,6 +102,14 @@
 
     def dev(seq_index, rep_index):
         return (section, seq_index, rep_index)
+
+    def nearest(step):
+        near = z + (step + 1) // 2 * (1 if step % 2 == 0 else -1)
+        far = jnp.where(2 * z < depth - 1, step, depth - 1 - step)
+        return jnp.where(step <= 2 * jnp.minimum(z, depth - 1 - z), near, far)
+
+    sources = [z] + [nearest(step) for step in range(1, depth)]
+    above, below = jnp.minimum(z + 1, depth - 1), jnp.maximum(z - 1, 0)
 
     def group_dev(step):
         other = lax.rem(group + step, groups)
@@ -113,16 +140,27 @@
     greet(peers + [(lax.rem(section + k, groups // n_rep), s, i) for k in range(1, groups // n_rep) for i in range(n_rep)])
     copies = Copies(send_sem)
 
+    def along(src, dst, sem):
+        copies.send(src, dst, sem, dev(above * 2 + y, r), when=z < depth - 1)
+        copies.send(src, dst, sem, dev(below * 2 + y, r), when=z > 0)
+
+    def onward(piece, sem, source):
+        up = source < z
+        device = dev(jnp.where(up, above, below) * 2 + y, r)
+        more = jnp.where(up, z < depth - 1, z > 0)
+        copies.send(piece, piece, sem, device, when=more)
+
     def spread(src, dst, sem):
+        along(src, dst.at[s], sem.at[s])
         copies.send(src, dst.at[s], sem.at[s], y_mate)
-        for k in range(1, depth):
-            copies.send(src, dst.at[s], sem.at[s], dev(at(k, y), r))
 
     def take(dst, sem, k, from_mate):
-        seq_index = at(depth - k, other_y if from_mate else y)
-        copies.arrived(dst.at[seq_index], sem.at[seq_index], y_mate)
+        seq_index = sources[k] * 2 + (other_y if from_mate else y)
+        piece = dst.at[seq_index]
+        copies.arrived(piece, sem.at[seq_index], y_mate)
         if not from_mate:
-            copies.send(dst.at[seq_index], dst.at[seq_index], sem.at[seq_index], y_mate)
+            onward(piece, sem.at[seq_index], sources[k])
+            copies.send(piece, piece, sem.at[seq_index], y_mate)
         return seq_index
 
     events = []
@@ -136,8 +174,10 @@
     spread(v_ref, values, v_sem)
     for k in range(1, depth):
         take(keys, k_sem, k, 0)
-    for k in range(1, depth):
         take(values, v_sem, k, 0)
+        if k == 1:
+            carried[...] = jnp.transpose(resid_ref[...].astype(jnp.float32))
+            bias[...] = mask_bias(order_ref, s, seq_dev, n_seq * seq_dev, block_rows)
     for copy in own:
         copy.wait()
     for k in range(depth):
@@ -151,7 +191,7 @@
         scores = lax.dot_general(
             q_ref[:, span], all_keys[:, span], (((1,), (1,)), ((), ())), preferred_element_type=jnp.float32
         )
-        scores = scores * HEAD_DIM**-0.5 + bias_ref[...]
+        scores = scores * HEAD_DIM**-0.5 + bias[...]
         prob = jnp.exp(scores - jnp.max(scores, axis=1, keepdims=True))
         totals.append(jnp.sum(prob, axis=1, keepdims=True))
         probs.append(prob.astype(jnp.bfloat16))
@@ -167,7 +207,7 @@
         proj[...] = jnp.dot(attended[seq_index], wo_ref[...], preferred_element_type=jnp.float32)
         proj_low[seq_index] = proj[...].astype(jnp.bfloat16)
         spot = pl.ds(pl.multiple_of(seq_index * sub, sub), sub)
-        carried[spot, :] = base_ref[spot, :] + proj[pl.ds(pl.multiple_of(group * sub, sub), sub), :]
+        carried[spot, :] += proj[pl.ds(pl.multiple_of(group * sub, sub), sub), :]
         for step in range(1, groups):
             other = lax.rem(group + step, groups)
             copies.send(
@@ -193,18 +233,17 @@
     carried[...] = total
     squares = jnp.sum(total * total, axis=1, keepdims=True)
     sq[s, r] = jnp.transpose(jnp.broadcast_to(squares, (tokens, tokens)))[:8]
-    x[s, rows(r), :] = (total * gain_ref[...]).astype(jnp.bfloat16)
-    for peer in peers:
-        copies.send(sq.at[s, r], sq.at[s, r], sq_sem.at[s, r], peer)
-
+    x[s, rows(r), :] = (total * gain_ref[...].astype(jnp.float32).reshape(1, columns)).astype(jnp.bfloat16)
     def forward(seq_index, device):
         piece = x.at[seq_index, rows(r), :]
         copies.send(piece, piece, x_sem.at[seq_index, r], device)
 
+    mine = x.at[s, rows(r), :]
+    along(mine, mine, x_sem.at[s, r])
     forward(s, y_mate)
-    for k in range(1, depth):
-        forward(s, dev(at(k, y), r))
     forward(s, rep_mate)
+    for peer in peers:
+        copies.send(sq.at[s, r], sq.at[s, r], sq_sem.at[s, r], peer)
 
     first = True
 
@@ -227,10 +266,11 @@
 
     pending = s
     for k, from_mate in events:
-        seq_index = at(depth - k, other_y if from_mate else y)
+        seq_index = sources[k] * 2 + (other_y if from_mate else y)
         piece = x.at[seq_index, rows(r), :]
         copies.arrived(piece, x_sem.at[seq_index, r], y_mate)
         if not from_mate:
+            onward(piece, x_sem.at[seq_index, r], sources[k])
             forward(seq_index, y_mate)
         forward(seq_index, rep_mate)
         accumulate(pending)
@@ -282,32 +322,33 @@
     for k in range(1, depth):
         copies.arrived(from_z.at[k - 1], z_sem.at[k - 1], y_mate)
         total += from_z[k - 1].astype(jnp.float32)
-    out_ref[...] = total.astype(jnp.bfloat16)
+    out_ref[...] = jnp.transpose(total).astype(jnp.bfloat16)
     copies.finish()
 
 
-def layer(q, k, v, bias, wo, base, gain, w_gate, w_up, w_down):
+def layer(order, q, k, v, wo, resid, gain, w_gate, w_up, w_down):
     n_seq, n_rep = lax.axis_size("seq"), lax.axis_size("rep")
     groups = n_rep * lax.axis_size("section")
     seq_dev, width = q.shape
-    tokens, columns = base.shape
+    columns, tokens = resid.shape
     features = w_gate.shape[1]
     half = w_gate.shape[0] // n_rep
     depth = n_seq // 2
-    sends = 3 * (n_seq - 1) + n_seq * (groups - 1) + (2 * n_seq - 1) * 2 + 2 * n_seq
+    sends = 3 * (n_seq + 1) + 2 + n_seq * (groups - 1) + (2 * n_seq - 1) * 2 + 2 * n_seq
     f32, bf16 = jnp.float32, jnp.bfloat16
     vmem = pl.BlockSpec(memory_space=pltpu.VMEM)
     hbm = pl.BlockSpec(memory_space=pl.ANY)
     dma = pltpu.SemaphoreType.DMA
     return pl.pallas_call(
         functools.partial(layer_kernel, n_seq, n_rep, groups),
-        out_shape=jax.ShapeDtypeStruct((tokens, columns), bf16),
-        in_specs=[vmem] * 7 + [hbm] * 3,
+        out_shape=jax.ShapeDtypeStruct((columns, tokens), bf16),
+        in_specs=[pl.BlockSpec(memory_space=pltpu.SMEM)] + [vmem] * 6 + [hbm] * 3,
         out_specs=vmem,
         scratch_shapes=[
             pltpu.VMEM((n_seq, seq_dev, width), bf16),
             pltpu.VMEM((n_seq, seq_dev, width), bf16),
             pltpu.VMEM((n_seq, seq_dev, width), bf16),
+            pltpu.VMEM((seq_dev, n_seq * seq_dev), f32),
             pltpu.VMEM((seq_dev, columns), f32),
             pltpu.VMEM((n_seq, seq_dev, columns), bf16),
             pltpu.VMEM((groups - 1, tokens, columns), bf16),
@@ -342,7 +383,7 @@
         compiler_params=pltpu.CompilerParams(
             collective_id=1, has_side_effects=True, vmem_limit_bytes=VMEM_BUDGET
         ),
-    )(q, k, v, bias, wo, base, gain, w_gate, w_up, w_down)
+    )(order, q, k, v, wo, resid, gain, w_gate, w_up, w_down)
 
 
 def kernels_fit(queries, wo, w_gate):
@@ -374,12 +415,9 @@
     query_start = lax.axis_index("seq") * seq_dev
     query_pos = key_positions(block_order, query_start, seq_dev, block_rows)
     if kernels_fit(queries, wo, w_gate):
-        key_pos = key_positions(block_order, jnp.int32(0), n_seq * seq_dev, block_rows)
-        bias = jnp.where(key_pos[None, :] <= query_pos[:, None], 0.0, -1e30).astype(jnp.float32)
-        base = resid.reshape(wo.shape[1], n_seq * sub_rows).T.astype(jnp.float32)
-        gain_row = gain.astype(jnp.float32)[None, :]
-        mixed = layer(queries, keys, values, bias, wo, base, gain_row, w_gate, w_up, w_down)
-        return mixed.T.reshape(resid.shape)
+        block = resid.reshape(wo.shape[1], n_seq * sub_rows)
+        mixed = layer(block_order, queries, keys, values, wo, block, gain, w_gate, w_up, w_down)
+        return mixed.reshape(resid.shape)
     query_heads = queries.reshape(seq_dev, heads_dev, HEAD_DIM)
     scale = HEAD_DIM ** (-0.5)
     running_max = jnp.full((seq_dev, heads_dev), -1e30, jnp.float32)

time: 104 us -> 93.1 us (0.90)
  Pallas kernels: 96.4 us -> 90.8 us
  other arithmetic: 2.99 us -> 0 us
  local copies, waits for them, and re-layouts: 4.06 us -> 1.59 us
    pallas_call x1, Pallas kernels: 96.4 us -> 90.8 us  [layer(): pl.pallas_call(functools.partial(layer_kernel, n_seq, n_rep, groups), out...]
    reshape x1 -> x0, local copies, waits for them, and re-layouts: 1.72 us -> none  [on_device(): return mixed.T.reshape(resid.shape)]
    reduce_sum x2 -> x0, other arithmetic: 1.49 us -> none  [key_positions(): first = jnp.sum(jnp.where(match, order[None, :], 0), axis=1)]
    broadcast_in_dim x1 -> x0, local copies, waits for them, and re-layouts: 1.28 us -> none  [on_device(): gain_row = gain.astype(jnp.float32)[None, :]]
where the time goes in v3:
time: 93.1 us; the launch traced here: 92.4 us
  Pallas kernels  90.8 us (98%)
  local copies, waits for them, and re-layouts  1.59 us (2%)
    pallas_call x1, Pallas kernels, layer(): pl.pallas_call(functools.partial(layer_kernel, n_seq, n_rep, groups), out...  90.8 us

profile of v3, /device:TPU:24, one launch (start us, length us, event | category | flops | bytes accessed | tf_op | source)
XLA Modules:
  0.0 92.4 jit_solution(10624167038384553236)
XLA Ops:
  0.0 90.8 %shard_map.100 = bf16[640,128]{1,0:T(8,128)(2,1)} custom-call(s32[16]{0:T(128)} %order_ref.1, bf16[64,640]{1,0:T(8,128)(2,1)} %q_ref.1, bf16[64,640]{1,0:T(8,128)(2,1)} %k_ref.1, bf16[64,640]{1,0:T(8,128)(2,1)} %v_ref.1, bf16[640,640]{1,0:T(8,128)(2,1)} %wo_ref.1, bf16[640,128]{1,0:T(8,128)(2,1)} %bitcast.3, bf16[640]{0:T(1024)(128)(2,1)} %gain_ref.1, ...), custom_call_target="tpu_custom_call" | custom-call | tf_op jit(solution)/shard_map/pallas_call | solution.py:342
  90.8 1.6 %copy.12 = bf16[1,640,128]{2,1,0:T(8,128)(2,1)} copy(bf16[1,640,128]{2,1,0:T(8,128)(2,1)} %bitcast.2) | data formatting | bytes 327680

commit v4 on v3

--- a/solution.py
+++ b/solution.py
@@ -20,6 +20,7 @@
 
 
 VMEM_BUDGET = 60 * 2**20
+PIECES = 2
 
 
 class Copies:
@@ -150,17 +151,22 @@
         more = jnp.where(up, z < depth - 1, z > 0)
         copies.send(piece, piece, sem, device, when=more)
 
+    seq_rows = seq_dev // PIECES
+
     def spread(src, dst, sem):
-        along(src, dst.at[s], sem.at[s])
-        copies.send(src, dst.at[s], sem.at[s], y_mate)
+        for p in range(PIECES):
+            span = pl.ds(p * seq_rows, seq_rows)
+            along(src.at[span, :], dst.at[s, span, :], sem.at[s, p])
+            copies.send(src.at[span, :], dst.at[s, span, :], sem.at[s, p], y_mate)
 
     def take(dst, sem, k, from_mate):
         seq_index = sources[k] * 2 + (other_y if from_mate else y)
-        piece = dst.at[seq_index]
-        copies.arrived(piece, sem.at[seq_index], y_mate)
-        if not from_mate:
-            onward(piece, sem.at[seq_index], sources[k])
-            copies.send(piece, piece, sem.at[seq_index], y_mate)
+        for p in range(PIECES):
+            piece = dst.at[seq_index, pl.ds(p * seq_rows, seq_rows), :]
+            copies.arrived(piece, sem.at[seq_index, p], y_mate)
+            if not from_mate:
+                onward(piece, sem.at[seq_index, p], sources[k])
+                copies.send(piece, piece, sem.at[seq_index, p], y_mate)
         return seq_index
 
     events = []
@@ -234,14 +240,20 @@
     squares = jnp.sum(total * total, axis=1, keepdims=True)
     sq[s, r] = jnp.transpose(jnp.broadcast_to(squares, (tokens, tokens)))[:8]
     x[s, rows(r), :] = (total * gain_ref[...].astype(jnp.float32).reshape(1, columns)).astype(jnp.bfloat16)
-    def forward(seq_index, device):
-        piece = x.at[seq_index, rows(r), :]
-        copies.send(piece, piece, x_sem.at[seq_index, r], device)
-
-    mine = x.at[s, rows(r), :]
-    along(mine, mine, x_sem.at[s, r])
-    forward(s, y_mate)
-    forward(s, rep_mate)
+    piece_rows = tokens // PIECES
+
+    def piece_of(seq_index, rep_index, p):
+        return x.at[seq_index, pl.ds(rep_index * tokens + p * piece_rows, piece_rows), :]
+
+    def forward(seq_index, p, device):
+        piece = piece_of(seq_index, r, p)
+        copies.send(piece, piece, x_sem.at[seq_index, r, p], device)
+
+    for p in range(PIECES):
+        mine = piece_of(s, r, p)
+        along(mine, mine, x_sem.at[s, r, p])
+        forward(s, p, y_mate)
+        forward(s, p, rep_mate)
     for peer in peers:
         copies.send(sq.at[s, r], sq.at[s, r], sq_sem.at[s, r], peer)
 
@@ -249,7 +261,8 @@
 
     def accumulate(seq_index):
         nonlocal first
-        copies.arrived(x.at[seq_index, rows(other_r), :], x_sem.at[seq_index, other_r], rep_mate)
+        for p in range(PIECES):
+            copies.arrived(piece_of(seq_index, other_r, p), x_sem.at[seq_index, other_r, p], rep_mate)
         block = x[seq_index]
         span = pl.ds(pl.multiple_of(seq_index * columns, 128), columns)
         for w, acc, load in ((w_gate, gate_acc, loads[0]), (w_up, up_acc, loads[1])):
@@ -267,12 +280,13 @@
     pending = s
     for k, from_mate in events:
         seq_index = sources[k] * 2 + (other_y if from_mate else y)
-        piece = x.at[seq_index, rows(r), :]
-        copies.arrived(piece, x_sem.at[seq_index, r], y_mate)
-        if not from_mate:
-            onward(piece, x_sem.at[seq_index, r], sources[k])
-            forward(seq_index, y_mate)
-        forward(seq_index, rep_mate)
+        for p in range(PIECES):
+            piece = piece_of(seq_index, r, p)
+            copies.arrived(piece, x_sem.at[seq_index, r, p], y_mate)
+            if not from_mate:
+                onward(piece, x_sem.at[seq_index, r, p], sources[k])
+                forward(seq_index, p, y_mate)
+            forward(seq_index, p, rep_mate)
         accumulate(pending)
         pending = seq_index
     for k in range(n_seq):
@@ -334,7 +348,8 @@
     features = w_gate.shape[1]
     half = w_gate.shape[0] // n_rep
     depth = n_seq // 2
-    sends = 3 * (n_seq + 1) + 2 + n_seq * (groups - 1) + (2 * n_seq - 1) * 2 + 2 * n_seq
+    blocks = PIECES * (3 * (1 + n_seq) + 4 + 2 * (depth - 1) + n_seq - 1)
+    sends = blocks + n_seq * (groups - 1) + (n_rep * n_seq - 1) + n_seq + 2 * depth - 1
     f32, bf16 = jnp.float32, jnp.bfloat16
     vmem = pl.BlockSpec(memory_space=pltpu.VMEM)
     hbm = pl.BlockSpec(memory_space=pl.ANY)
@@ -370,11 +385,11 @@
             dma((3,)),
             dma((2,)),
             dma((sends,)),
-            dma((n_seq,)),
-            dma((n_seq,)),
-            dma((n_seq,)),
+            dma((n_seq, PIECES)),
+            dma((n_seq, PIECES)),
+            dma((n_seq, PIECES)),
             dma((groups - 1, n_seq)),
-            dma((n_seq, n_rep)),
+            dma((n_seq, n_rep, PIECES)),
             dma((n_seq, n_rep)),
             dma((n_seq,)),
             dma((depth,)),
@@ -400,6 +415,7 @@
         and columns % 128 == 0
         and tokens % 128 == 0
         and sub % 16 == 0
+        and queries.shape[0] % (16 * PIECES) == 0
         and half % 16 == 0
         and held < VMEM_BUDGET - 8 * 2**20
     )

time: 93.1 us -> 92.1 us (0.989)
  no operation moved by 1% of the time
where the time goes in v4:
time: 92.1 us; the launch traced here: 91.5 us
  Pallas kernels  89.9 us (98%)
  local copies, waits for them, and re-layouts  1.59 us (2%)
    pallas_call x1, Pallas kernels, layer(): pl.pallas_call(functools.partial(layer_kernel, n_seq, n_rep, groups), out...  89.9 us

profile of v4, /device:TPU:24, one launch (start us, length us, event | category | flops | bytes accessed | tf_op | source)
XLA Modules:
  0.0 91.5 jit_solution(6047191961648604699)
XLA Ops:
  0.0 89.9 %shard_map.100 = bf16[640,128]{1,0:T(8,128)(2,1)} custom-call(s32[16]{0:T(128)} %order_ref.1, bf16[64,640]{1,0:T(8,128)(2,1)} %q_ref.1, bf16[64,640]{1,0:T(8,128)(2,1)} %k_ref.1, bf16[64,640]{1,0:T(8,128)(2,1)} %v_ref.1, bf16[640,640]{1,0:T(8,128)(2,1)} %wo_ref.1, bf16[640,128]{1,0:T(8,128)(2,1)} %bitcast.3, bf16[640]{0:T(1024)(128)(2,1)} %gain_ref.1, ...), custom_call_target="tpu_custom_call" | custom-call | tf_op jit(solution)/shard_map/pallas_call | solution.py:357
  89.9 1.6 %copy.12 = bf16[1,640,128]{2,1,0:T(8,128)(2,1)} copy(bf16[1,640,128]{2,1,0:T(8,128)(2,1)} %bitcast.2) | data formatting | bytes 327680

commit v5 on v4

--- a/solution.py
+++ b/solution.py
@@ -269,7 +269,7 @@
             if first:
                 load.wait()
             term = lax.dot_general(
-                block, w[:, span], (((1,), (1,)), ((), ())), preferred_element_type=jnp.float32
+                w[:, span], block, (((1,), (1,)), ((), ())), preferred_element_type=jnp.float32
             )
             if first:
                 acc[...] = term
@@ -298,12 +298,11 @@
 
     for rep_index in range(2):
         total = jnp.sum(sq[:, rep_index], axis=0)
-        factor = lax.rsqrt(total / (n_seq * columns) + 1e-05)
-        factor = jnp.transpose(factor)[:, :1]
-        own_rows = slice(rep_index * tokens, (rep_index + 1) * tokens)
-        gate = gate_acc[own_rows, :] * factor
-        up = up_acc[own_rows, :] * factor
-        hidden[own_rows, :] = (gate / (1.0 + jnp.exp(-gate)) * up).astype(jnp.bfloat16)
+        factor = lax.rsqrt(total / (n_seq * columns) + 1e-05)[:1]
+        span = slice(rep_index * tokens, (rep_index + 1) * tokens)
+        gate = gate_acc[:, span] * factor
+        up = up_acc[:, span] * factor
+        hidden[span, :] = jnp.transpose(gate / (1.0 + jnp.exp(-gate)) * up).astype(jnp.bfloat16)
     loads[2].wait()
 
     order = [(k % depth, 1) for k in range(1, depth + 1)] + [(k % depth, 0) for k in range(1, depth + 1)]
@@ -373,8 +372,8 @@
             pltpu.VMEM((half, features), bf16),
             pltpu.VMEM((half, features), bf16),
             pltpu.VMEM((half, features), bf16),
-            pltpu.VMEM((n_rep * tokens, half), f32),
-            pltpu.VMEM((n_rep * tokens, half), f32),
+            pltpu.VMEM((half, n_rep * tokens), f32),
+            pltpu.VMEM((half, n_rep * tokens), f32),
             pltpu.VMEM((n_rep * tokens, half), bf16),
             pltpu.VMEM((n_seq, n_rep * tokens, columns), f32),
             pltpu.VMEM((n_seq, tokens, columns), f32),

time: 92.1 us -> 91.8 us (level)
  no operation moved by 1% of the time
where the time goes in v5:
time: 91.8 us; the launch traced here: 91.1 us
  Pallas kernels  89.5 us (97%)
  local copies, waits for them, and re-layouts  1.59 us (2%)
    pallas_call x1, Pallas kernels, layer(): pl.pallas_call(functools.partial(layer_kernel, n_seq, n_rep, groups), out...  89.5 us

profile of v5, /device:TPU:24, one launch (start us, length us, event | category | flops | bytes accessed | tf_op | source)
XLA Modules:
  0.0 91.1 jit_solution(12411334359805154447)
XLA Ops:
  0.0 89.5 %shard_map.100 = bf16[640,128]{1,0:T(8,128)(2,1)} custom-call(s32[16]{0:T(128)} %order_ref.1, bf16[64,640]{1,0:T(8,128)(2,1)} %q_ref.1, bf16[64,640]{1,0:T(8,128)(2,1)} %k_ref.1, bf16[64,640]{1,0:T(8,128)(2,1)} %v_ref.1, bf16[640,640]{1,0:T(8,128)(2,1)} %wo_ref.1, bf16[640,128]{1,0:T(8,128)(2,1)} %bitcast.3, bf16[640]{0:T(1024)(128)(2,1)} %gain_ref.1, ...), custom_call_target="tpu_custom_call" | custom-call | tf_op jit(solution)/shard_map/pallas_call | solution.py:356
  89.5 1.6 %copy.12 = bf16[1,640,128]{2,1,0:T(8,128)(2,1)} copy(bf16[1,640,128]{2,1,0:T(8,128)(2,1)} %bitcast.2) | data formatting | bytes 327680
